TPU v7x, 32 devices: a whole 2x2x4 slice. The times are simulated.
32 devices in a mesh: gx: 4 (over z), gy: 8 (over y, x, core).
Axes of the slice: x: 2, y: 2, z: 4, core: 2. Of those that a mesh axis runs over, the one named last changes fastest.
Arguments:
- probes: float32 [8, 64, 128, 512], P(None, 'gx', 'gy'), may hold values from -12.5 to 12.5, as said below
- disorder: float32 [64, 128, 512], P('gx', 'gy'), may hold values from -2 to 2
- spectrum_center: float32 [1], replicated, may hold values from -0.5 to 0.5
- half_width: float32 [1], replicated, may hold values from 9 to 11
Outputs:
- last_vector: float32 [8, 64, 128, 512], P(None, 'gx', 'gy')
- moments: float32 [8, 8], replicated
Inputs may be any that keep to these rules, and one draw needn't show every extreme that they name: `probes`: real-valued probe entries.
All inputs are finite; a program needn't handle non-finite values.
Results may differ from a plain program's by a relative error of at most 0.0001.
Values sent between devices are 32-bit elements; how exact they have to be, the bound alone decides.
A program may use at most 128 MiB of HBM per device.

v0:
```python
import jax
import jax.numpy as jnp
from jax import lax
from jax.sharding import PartitionSpec as P

STEPS = 4


def extended(block, sides, width):
    for axis, dim in sides:
        count = lax.axis_size(axis)
        forward = [(i, i + 1) for i in range(count - 1)]
        forward.append((count - 1, 0))
        backward = [(target, source) for source, target in forward]
        low = lax.ppermute(
            lax.slice_in_dim(block, block.shape[dim] - width, None, axis=dim), axis, forward
        )
        high = lax.ppermute(lax.slice_in_dim(block, 0, width, axis=dim), axis, backward)
        block = jnp.concatenate([low, block, high], axis=dim)
    return block


def scaled_apply(ext, eps_part, center, width):
    core = ext[:, 1:-1, 1:-1]
    beside = ext[:, 2:, 1:-1] + ext[:, :-2, 1:-1] + ext[:, 1:-1, 2:] + ext[:, 1:-1, :-2]
    beside = beside + jnp.roll(core, 1, 3) + jnp.roll(core, -1, 3)
    return ((eps_part - center) * core - beside) / width


def inner_pair(t_low, t_high):
    square = jnp.sum(t_low * t_low, axis=(1, 2, 3))
    cross = jnp.sum(t_high * t_low, axis=(1, 2, 3))
    return jnp.stack([square, cross])


def with_rim(field):
    return extended(field, (("gx", 1), ("gy", 2)), 1)


def local(probes, disorder, spectrum_center, half_width):
    center = spectrum_center[0]
    width = half_width[0]
    energy = disorder[None]
    collected = []

    def keep(pair):
        collected.append(pair)

    t_low = probes
    t_high = scaled_apply(with_rim(t_low), energy, center, width)
    for step in range(STEPS):
        keep(inner_pair(t_low, t_high))
        if step + 1 < STEPS:
            t_next = 2.0 * scaled_apply(with_rim(t_high), energy, center, width) - t_low
            t_low, t_high = (t_high, t_next)
    stacked = jnp.stack(collected)
    stacked = lax.psum(stacked, ("gx", "gy"))
    total_sites = (
        probes.shape[1]
        * lax.axis_size("gx")
        * probes.shape[2]
        * lax.axis_size("gy")
        * probes.shape[3]
    )
    sites = jnp.float32(total_sites)
    square = stacked[:, 0, :] / sites
    cross = stacked[:, 1, :] / sites
    even = 2.0 * square - square[0]
    odd = 2.0 * cross - cross[0]
    moments = jnp.stack([even, odd], axis=1).reshape(2 * STEPS, -1).T
    return (t_high, moments)


def solution(mesh):
    in_specs = (P(None, "gx", "gy", None), P("gx", "gy", None), P(), P())
    out_specs = (P(None, "gx", "gy", None), P())
    return jax.shard_map(local, mesh=mesh, in_specs=in_specs, out_specs=out_specs, check_vma=False)
```

profile of v0, /device:TPU:0, one launch (start us, length us, event | category | flops | bytes accessed | tf_op | source)
XLA Modules:
  0.0 198.8 jit_solution(14120249625105281826)
XLA Ops:
  0.6 5.4 %copy.7 = f32[8,16,16,512]{3,0,2,1:T(8,128)S(1)} copy(f32[8,16,16,512]{3,2,1,0:T(8,128)} %param.4) | data formatting | bytes 8388608 | tf_op args[0]
  6.1 3.1 %collective-permute-start.1 = (f32[8,1,16,512]{3,0,2,1:T(8,128)S(1)}, f32[8,1,16,512]{3,0,2,1:T(8,128)S(1)}, u32[]{:S(2)}, u32[]{:S(2)}) collective-permute-start(f32[8,1,16,512]{3,0,2,1:T(8,128)S(1)} %get-tuple-element.45), channel_id=1, source_target_pairs={{0,8},{8,16},{16,24},{24,0},{1,9},{9,17},{17,25},{25,1},{2,10},{10... | collective-permute-start | bytes 786440 | tf_op jit(solution)/shard_map/ppermute | solution.py:15
  9.2 2.1 %collective-permute-start = (f32[8,1,16,512]{3,0,2,1:T(8,128)S(1)}, f32[8,1,16,512]{3,0,2,1:T(8,128)S(1)}, u32[]{:S(2)}, u32[]{:S(2)}) collective-permute-start(f32[8,1,16,512]{3,0,2,1:T(8,128)S(1)} %get-tuple-element.44), channel_id=1, source_target_pairs={{8,0},{16,8},{24,16},{0,24},{9,1},{17,9},{25,17},{1,25},{10,2},{18... | collective-permute-start | bytes 786440 | tf_op jit(solution)/shard_map/ppermute | solution.py:18
  11.3 3.5 %fusion.47 = (f32[8,16,16,511]{3,0,2,1:T(8,128)S(1)}, f32[8,16,16,511]{3,0,2,1:T(8,128)}) fusion(f32[8,16,16,512]{3,0,2,1:T(8,128)S(1)} %copy.7), kind=kLoop, calls=%fused_computation.105 | loop fusion | bytes 16744448 | tf_op jit(solution)/shard_map/jit(_roll_static)/slice | solution.py:26
  16.1 0.0 copy-done.7
  16.2 0.0 copy-done.1
  16.2 0.5 multiply_reduce_fusion.7
  16.7 1.8 collective-permute-done.1
  18.5 3.3 %constant_dynamic-update-slice_fusion.1 = f32[8,18,16,512]{3,0,2,1:T(8,128)S(1)} fusion(f32[8,18,16,512]{3,0,2,1:T(8,128)S(1)} %constant_dynamic-update-slice_fusion.2, f32[8,16,16,512]{3,2,1,0:T(8,128)S(1)} %copy-done.1), kind=kLoop, calls=%fused_computation.81 | loop fusion | bytes 8388608
  21.7 0.9 collective-permute-done
  22.6 0.0 copy-start.3
  22.7 1.6 collective-permute-start.2
  24.2 0.0 copy-done.4
  24.3 0.0 collective-permute-start.3
  24.3 0.4 fusion.48
  24.7 7.0 %collective-permute-done.2 = f32[8,18,1,512]{3,0,2,1:T(8,128)S(1)} collective-permute-done((f32[8,18,1,512]{3,0,2,1:T(8,128)S(1)}, f32[8,18,1,512]{3,0,2,1:T(8,128)S(1)}, u32[]{:S(2)}, u32[]{:S(2)}) %collective-permute-start.2) | collective-permute-done | bytes 294944 | tf_op jit(solution)/shard_map/ppermute | solution.py:18
  31.6 1.4 collective-permute-done.3
  33.1 0.0 copy-done.3
  33.1 0.0 copy-done.8
  33.1 0.7 copy-done.11
  33.8 8.1 %fusion.31 = f32[8,16,16,512]{3,0,2,1:T(8,128)S(1)} fusion(f32[8,18,16,512]{3,0,2,1:T(8,128)} %copy-done.3, f32[8,18,1,512]{3,0,2,1:T(8,128)} %copy-done.11, f32[8,18,1,512]{3,0,2,1:T(8,128)} %copy-done.8, f32[8,16,16,512]{3,0,2,1:T(8,128)S(1)} %copy.7, f32[8,1,16,512]{3,0,2,1:T(8,128)S(1)} %collective-permute-done.1, f32[8,1,16,512]{3,0,2,1:T(8,128)} %copy-done.4, ...), kind=kLoop, calls=%fused_computation.56 | loop fusion | flops 14680064 | bytes 23134212 | tf_op jit(solution)/shard_map/div | solution.py:27
  41.9 5.7 %collective-permute-start.4 = (f32[8,1,16,512]{3,0,2,1:T(8,128)S(1)}, f32[8,1,16,512]{3,0,2,1:T(8,128)S(1)}, u32[]{:S(2)}, u32[]{:S(2)}) collective-permute-start(f32[8,1,16,512]{3,0,2,1:T(8,128)S(1)} %get-tuple-element.39), channel_id=1, source_target_pairs={{8,0},{16,8},{24,16},{0,24},{9,1},{17,9},{25,17},{1,25},{10,2},{18... | collective-permute-start | bytes 786440 | tf_op jit(solution)/shard_map/ppermute | solution.py:18
  47.5 0.0 collective-permute-start.5
  47.6 4.8 %fusion.44 = (f32[8,16,16,511]{3,0,2,1:T(8,128)}, f32[8,16,16,511]{3,0,2,1:T(8,128)}) fusion(f32[8,16,16,512]{3,0,2,1:T(8,128)S(1)} %fusion.31), kind=kLoop, calls=%fused_computation.102 | loop fusion | bytes 16744448 | tf_op jit(solution)/shard_map/jit(_roll_static)/slice | solution.py:26
  52.4 1.5 collective-permute-done.4
  53.9 4.0 %collective-permute-done.5 = f32[8,1,16,512]{3,0,2,1:T(8,128)S(1)} collective-permute-done((f32[8,1,16,512]{3,0,2,1:T(8,128)S(1)}, f32[8,1,16,512]{3,0,2,1:T(8,128)S(1)}, u32[]{:S(2)}, u32[]{:S(2)}) %collective-permute-start.5) | collective-permute-done | bytes 262176 | tf_op jit(solution)/shard_map/ppermute | solution.py:15
  57.9 0.1 collective-permute-start.6
  58.0 0.6 copy-done.5
  58.6 0.0 collective-permute-start.7
  58.6 0.4 fusion.45
  59.0 5.5 %collective-permute-done.6 = f32[8,18,1,512]{3,0,2,1:T(8,128)S(1)} collective-permute-done((f32[8,18,1,512]{3,0,2,1:T(8,128)S(1)}, f32[8,18,1,512]{3,0,2,1:T(8,128)S(1)}, u32[]{:S(2)}, u32[]{:S(2)}) %collective-permute-start.6) | collective-permute-done | bytes 294944 | tf_op jit(solution)/shard_map/ppermute | solution.py:18
  64.4 3.6 %collective-permute-done.7 = f32[8,18,1,512]{3,0,2,1:T(8,128)S(1)} collective-permute-done((f32[8,18,1,512]{3,0,2,1:T(8,128)S(1)}, f32[8,18,1,512]{3,0,2,1:T(8,128)S(1)}, u32[]{:S(2)}, u32[]{:S(2)}) %collective-permute-start.7) | collective-permute-done | bytes 294944 | tf_op jit(solution)/shard_map/ppermute | solution.py:15
  68.1 0.0 copy-done.9
  68.1 0.7 copy-done.12
  68.8 12.0 %fusion.24 = f32[8,16,16,512]{3,0,2,1:T(8,128)S(1)} fusion(f32[8,18,1,512]{3,0,2,1:T(8,128)} %copy-done.12, f32[8,1,16,512]{3,0,2,1:T(8,128)S(1)} %collective-permute-done.4, f32[8,16,16,512]{3,0,2,1:T(8,128)S(1)} %fusion.31, f32[8,1,16,512]{3,0,2,1:T(8,128)} %copy-done.5, f32[8,18,1,512]{3,0,2,1:T(8,128)} %copy-done.9, ...), kind=kLoop, calls=%fused_computation.41 | loop fusion | flops 20971520 | bytes 22609924 | tf_op jit(solution)/shard_map/sub | solution.py:54
  80.9 1.5 collective-permute-start.8
  82.4 0.6 collective-permute-start.9
  83.0 4.9 %fusion.41 = (f32[8,16,16,511]{3,0,2,1:T(8,128)}, f32[8,16,16,511]{3,0,2,1:T(8,128)}) fusion(f32[8,16,16,512]{3,0,2,1:T(8,128)S(1)} %fusion.24), kind=kLoop, calls=%fused_computation.99 | loop fusion | bytes 16744448 | tf_op jit(solution)/shard_map/jit(_roll_static)/slice | solution.py:26
  87.9 1.8 collective-permute-done.8
  89.7 2.8 %collective-permute-done.9 = f32[8,1,16,512]{3,0,2,1:T(8,128)S(1)} collective-permute-done((f32[8,1,16,512]{3,0,2,1:T(8,128)S(1)}, f32[8,1,16,512]{3,0,2,1:T(8,128)S(1)}, u32[]{:S(2)}, u32[]{:S(2)}) %collective-permute-start.9) | collective-permute-done | bytes 262176 | tf_op jit(solution)/shard_map/ppermute | solution.py:15
  92.5 0.1 collective-permute-start.10
  92.6 0.6 copy-done.6
  93.2 0.0 collective-permute-start.11
  93.2 0.4 fusion.42
  93.6 4.3 %collective-permute-done.10 = f32[8,18,1,512]{3,0,2,1:T(8,128)S(1)} collective-permute-done((f32[8,18,1,512]{3,0,2,1:T(8,128)S(1)}, f32[8,18,1,512]{3,0,2,1:T(8,128)S(1)}, u32[]{:S(2)}, u32[]{:S(2)}) %collective-permute-start.10) | collective-permute-done | bytes 294944 | tf_op jit(solution)/shard_map/ppermute | solution.py:18
  97.9 5.3 %collective-permute-done.11 = f32[8,18,1,512]{3,0,2,1:T(8,128)S(1)} collective-permute-done((f32[8,18,1,512]{3,0,2,1:T(8,128)S(1)}, f32[8,18,1,512]{3,0,2,1:T(8,128)S(1)}, u32[]{:S(2)}, u32[]{:S(2)}) %collective-permute-start.11) | collective-permute-done | bytes 294944 | tf_op jit(solution)/shard_map/ppermute | solution.py:15
  103.2 0.0 copy-done.10
  103.2 0.7 copy-done.13
  103.9 9.0 %fusion.15 = f32[8,16,16,512]{3,0,2,1:T(8,128)} fusion(f32[8,16,16,512]{3,0,2,1:T(8,128)S(1)} %fusion.31, f32[8,18,1,512]{3,0,2,1:T(8,128)} %copy-done.13, f32[8,1,16,512]{3,0,2,1:T(8,128)S(1)} %collective-permute-done.8, f32[8,16,16,512]{3,0,2,1:T(8,128)S(1)} %fusion.24, f32[8,1,16,512]{3,0,2,1:T(8,128)} %copy-done.6, f32[8,18,1,512]{3,0,2,1:T(8,128)} %copy-done.10, ...), kind=kLoop, calls=%fused_computation.24 | loop fusion | flops 20971520 | bytes 22609924 | tf_op jit(solution)/shard_map/sub | solution.py:54
  113.0 1.1 fusion.38
  114.0 3.1 %collective-permute-start.12 = (f32[8,1,16,512]{3,0,2,1:T(8,128)S(1)}, f32[8,1,16,512]{3,0,2,1:T(8,128)S(1)}, u32[]{:S(2)}, u32[]{:S(2)}) collective-permute-start(f32[8,1,16,512]{3,0,2,1:T(8,128)S(1)} %get-tuple-element.23), channel_id=1, source_target_pairs={{8,0},{16,8},{24,16},{0,24},{9,1},{17,9},{25,17},{1,25},{10,2},{18... | collective-permute-start | bytes 786440 | tf_op jit(solution)/shard_map/ppermute | solution.py:18
  117.1 0.0 collective-permute-start.13
  117.1 8.2 %fusion.40 = (f32[8,16,16,511]{3,0,2,1:T(8,128)}, f32[8,16,16,511]{3,0,2,1:T(8,128)}) fusion(f32[8,16,16,512]{3,0,2,1:T(8,128)} %fusion.15), kind=kLoop, calls=%fused_computation.98 | loop fusion | bytes 16744448 | tf_op jit(solution)/shard_map/jit(_roll_static)/slice | solution.py:26
  125.3 0.0 collective-permute-done.12
  125.3 3.4 %collective-permute-done.13 = f32[8,1,16,512]{3,0,2,1:T(8,128)S(1)} collective-permute-done((f32[8,1,16,512]{3,0,2,1:T(8,128)S(1)}, f32[8,1,16,512]{3,0,2,1:T(8,128)S(1)}, u32[]{:S(2)}, u32[]{:S(2)}) %collective-permute-start.13) | collective-permute-done | bytes 262176 | tf_op jit(solution)/shard_map/ppermute | solution.py:15
  128.8 0.1 collective-permute-start.14
  128.8 0.5 collective-permute-start.15
  129.3 0.4 fusion.39
  129.7 5.7 %collective-permute-done.14 = f32[8,18,1,512]{3,0,2,1:T(8,128)S(1)} collective-permute-done((f32[8,18,1,512]{3,0,2,1:T(8,128)S(1)}, f32[8,18,1,512]{3,0,2,1:T(8,128)S(1)}, u32[]{:S(2)}, u32[]{:S(2)}) %collective-permute-start.14) | collective-permute-done | bytes 294944 | tf_op jit(solution)/shard_map/ppermute | solution.py:18
  135.4 2.7 %collective-permute-done.15 = f32[8,18,1,512]{3,0,2,1:T(8,128)S(1)} collective-permute-done((f32[8,18,1,512]{3,0,2,1:T(8,128)S(1)}, f32[8,18,1,512]{3,0,2,1:T(8,128)S(1)}, u32[]{:S(2)}, u32[]{:S(2)}) %collective-permute-start.15) | collective-permute-done | bytes 294944 | tf_op jit(solution)/shard_map/ppermute | solution.py:15
  138.2 13.2 %multiply_reduce_fusion.6 = (f32[8]{0:T(128)S(1)}, f32[8]{0:T(128)S(1)}, f32[8]{0:T(128)S(1)}, f32[8]{0:T(128)S(1)}, f32[8]{0:T(128)S(1)}, /*index=5*/f32[8]{0:T(128)S(1)}, f32[8]{0:T(128)S(1)}, f32[8,16,16,512]{3,0,2,1:T(8,128)}) fusion(f32[8,16,16,512]{3,0,2,1:T(8,128)S(1)} %fusion.31, f32[8,16,16,512]{3,2,1,0:T(8,128)S(1)} %copy-done.2, ...), kind=kLoop, calls=%fused_computation.68 | loop fusion | flops 35651528 | bytes 30998756 | tf_op jit(solution)/shard_map/reduce_sum | solution.py:32
  151.4 40.1 %psum.7 = f32[4,2,8]{2,1,0:T(2,128)S(1)} all-reduce(f32[4,2,8]{2,1,0:T(2,128)S(1)} %pad_maximum_fusion.37), channel_id=1, replica_groups=mesh['gx'=4,'gy'=8] {'gx','gy'}, use_global_device_ids=true, to_apply=%region_8.9 | all-reduce | flops 64 | bytes 512 | tf_op jit(solution)/shard_map/psum | solution.py:57
  191.5 0.7 copy.20
  192.2 6.6 %copy.19 = f32[8,16,16,512]{3,2,1,0:T(8,128)} copy(f32[8,16,16,512]{3,0,2,1:T(8,128)} %get-tuple-element.13) | data formatting | bytes 8388608
  (33 shorter events, 0.4 us)
Async XLA Ops:
  6.1 12.3 %collective-permute-start.1 = (f32[8,1,16,512]{3,0,2,1:T(8,128)S(1)}, f32[8,1,16,512]{3,0,2,1:T(8,128)S(1)}, u32[]{:S(2)}, u32[]{:S(2)}) collective-permute-start(f32[8,1,16,512]{3,0,2,1:T(8,128)S(1)} %get-tuple-element.45), channel_id=1, source_target_pairs={{0,8},{8,16},{16,24},{24,0},{1,9},{9,17},{17,25},{25,1},{2,10},{10... | collective-permute-start | bytes 786440 | tf_op jit(solution)/shard_map/ppermute | solution.py:15
  9.2 6.9 %copy-start.7 = (f32[16,16,512]{2,1,0:T(8,128)S(1)}, f32[16,16,512]{2,1,0:T(8,128)}, u32[]{:S(2)}) copy-start(f32[16,16,512]{2,1,0:T(8,128)} %param.5) | copy-start | bytes 1572868
  9.2 7.0 %copy-start.1 = (f32[8,16,16,512]{3,2,1,0:T(8,128)S(1)}, f32[8,16,16,512]{3,2,1,0:T(8,128)}, u32[]{:S(2)}) copy-start(f32[8,16,16,512]{3,2,1,0:T(8,128)} %param.4) | copy-start | bytes 12582916
  9.2 13.4 %collective-permute-start = (f32[8,1,16,512]{3,0,2,1:T(8,128)S(1)}, f32[8,1,16,512]{3,0,2,1:T(8,128)S(1)}, u32[]{:S(2)}, u32[]{:S(2)}) collective-permute-start(f32[8,1,16,512]{3,0,2,1:T(8,128)S(1)} %get-tuple-element.44), channel_id=1, source_target_pairs={{8,0},{16,8},{24,16},{0,24},{9,1},{17,9},{25,17},{1,25},{10,2},{18... | collective-permute-start | bytes 786440 | tf_op jit(solution)/shard_map/ppermute | solution.py:18
  22.6 1.6 copy-start.4
  22.6 10.4 %copy-start.3 = (f32[8,18,16,512]{3,0,2,1:T(8,128)}, f32[8,18,16,512]{3,0,2,1:T(8,128)S(1)}, u32[]{:S(2)}) copy-start(f32[8,18,16,512]{3,0,2,1:T(8,128)S(1)} %constant_dynamic-update-slice_fusion) | copy-start | bytes 14155780
  22.7 8.9 %collective-permute-start.2 = (f32[8,18,1,512]{3,0,2,1:T(8,128)S(1)}, f32[8,18,1,512]{3,0,2,1:T(8,128)S(1)}, u32[]{:S(2)}, u32[]{:S(2)}) collective-permute-start(f32[8,18,1,512]{3,0,2,1:T(8,128)S(1)} %get-tuple-element.20), channel_id=1, source_target_pairs={{1,0},{2,1},{3,2},{4,3},{5,4},{6,5},{7,6},{0,7},{9,8},{10,9},{11,1... | collective-permute-start | bytes 884744 | tf_op jit(solution)/shard_map/ppermute | solution.py:18
  24.3 8.8 %collective-permute-start.3 = (f32[8,18,1,512]{3,0,2,1:T(8,128)S(1)}, f32[8,18,1,512]{3,0,2,1:T(8,128)S(1)}, u32[]{:S(2)}, u32[]{:S(2)}) collective-permute-start(f32[8,18,1,512]{3,0,2,1:T(8,128)S(1)} %get-tuple-element.21), channel_id=1, source_target_pairs={{0,1},{1,2},{2,3},{3,4},{4,5},{5,6},{6,7},{7,0},{8,9},{9,10},{10,1... | collective-permute-start | bytes 884744 | tf_op jit(solution)/shard_map/ppermute | solution.py:15
  31.6 1.4 copy-start.8
  33.1 0.7 copy-start.11
  41.9 12.0 %collective-permute-start.4 = (f32[8,1,16,512]{3,0,2,1:T(8,128)S(1)}, f32[8,1,16,512]{3,0,2,1:T(8,128)S(1)}, u32[]{:S(2)}, u32[]{:S(2)}) collective-permute-start(f32[8,1,16,512]{3,0,2,1:T(8,128)S(1)} %get-tuple-element.39), channel_id=1, source_target_pairs={{8,0},{16,8},{24,16},{0,24},{9,1},{17,9},{25,17},{1,25},{10,2},{18... | collective-permute-start | bytes 786440 | tf_op jit(solution)/shard_map/ppermute | solution.py:18
  47.5 10.3 %collective-permute-start.5 = (f32[8,1,16,512]{3,0,2,1:T(8,128)S(1)}, f32[8,1,16,512]{3,0,2,1:T(8,128)S(1)}, u32[]{:S(2)}, u32[]{:S(2)}) collective-permute-start(f32[8,1,16,512]{3,0,2,1:T(8,128)S(1)} %get-tuple-element.38), channel_id=1, source_target_pairs={{0,8},{8,16},{16,24},{24,0},{1,9},{9,17},{17,25},{25,1},{2,10},{10... | collective-permute-start | bytes 786440 | tf_op jit(solution)/shard_map/ppermute | solution.py:15
  57.9 0.7 copy-start.5
  57.9 6.5 %collective-permute-start.6 = (f32[8,18,1,512]{3,0,2,1:T(8,128)S(1)}, f32[8,18,1,512]{3,0,2,1:T(8,128)S(1)}, u32[]{:S(2)}, u32[]{:S(2)}) collective-permute-start(f32[8,18,1,512]{3,0,2,1:T(8,128)S(1)} %get-tuple-element.18), channel_id=1, source_target_pairs={{1,0},{2,1},{3,2},{4,3},{5,4},{6,5},{7,6},{0,7},{9,8},{10,9},{11,1... | collective-permute-start | bytes 884744 | tf_op jit(solution)/shard_map/ppermute | solution.py:18
  58.6 9.5 %collective-permute-start.7 = (f32[8,18,1,512]{3,0,2,1:T(8,128)S(1)}, f32[8,18,1,512]{3,0,2,1:T(8,128)S(1)}, u32[]{:S(2)}, u32[]{:S(2)}) collective-permute-start(f32[8,18,1,512]{3,0,2,1:T(8,128)S(1)} %get-tuple-element.19), channel_id=1, source_target_pairs={{0,1},{1,2},{2,3},{3,4},{4,5},{5,6},{6,7},{7,0},{8,9},{9,10},{10,1... | collective-permute-start | bytes 884744 | tf_op jit(solution)/shard_map/ppermute | solution.py:15
  64.4 3.6 %copy-start.9 = (f32[8,18,1,512]{3,0,2,1:T(8,128)}, f32[8,18,1,512]{3,0,2,1:T(8,128)S(1)}, u32[]{:S(2)}) copy-start(f32[8,18,1,512]{3,0,2,1:T(8,128)S(1)} %collective-permute-done.6) | copy-start | bytes 884740
  68.1 0.7 copy-start.12
  80.9 8.8 %collective-permute-start.8 = (f32[8,1,16,512]{3,0,2,1:T(8,128)S(1)}, f32[8,1,16,512]{3,0,2,1:T(8,128)S(1)}, u32[]{:S(2)}, u32[]{:S(2)}) collective-permute-start(f32[8,1,16,512]{3,0,2,1:T(8,128)S(1)} %get-tuple-element.33), channel_id=1, source_target_pairs={{8,0},{16,8},{24,16},{0,24},{9,1},{17,9},{25,17},{1,25},{10,2},{18... | collective-permute-start | bytes 786440 | tf_op jit(solution)/shard_map/ppermute | solution.py:18
  82.4 10.1 %collective-permute-start.9 = (f32[8,1,16,512]{3,0,2,1:T(8,128)S(1)}, f32[8,1,16,512]{3,0,2,1:T(8,128)S(1)}, u32[]{:S(2)}, u32[]{:S(2)}) collective-permute-start(f32[8,1,16,512]{3,0,2,1:T(8,128)S(1)} %get-tuple-element.32), channel_id=1, source_target_pairs={{0,8},{8,16},{16,24},{24,0},{1,9},{9,17},{17,25},{25,1},{2,10},{10... | collective-permute-start | bytes 786440 | tf_op jit(solution)/shard_map/ppermute | solution.py:15
  92.5 0.7 copy-start.6
  92.5 5.4 %collective-permute-start.10 = (f32[8,18,1,512]{3,0,2,1:T(8,128)S(1)}, f32[8,18,1,512]{3,0,2,1:T(8,128)S(1)}, u32[]{:S(2)}, u32[]{:S(2)}) collective-permute-start(f32[8,18,1,512]{3,0,2,1:T(8,128)S(1)} %get-tuple-element.16), channel_id=1, source_target_pairs={{1,0},{2,1},{3,2},{4,3},{5,4},{6,5},{7,6},{0,7},{9,8},{10,9},{11,1... | collective-permute-start | bytes 884744 | tf_op jit(solution)/shard_map/ppermute | solution.py:18
  93.2 10.0 %collective-permute-start.11 = (f32[8,18,1,512]{3,0,2,1:T(8,128)S(1)}, f32[8,18,1,512]{3,0,2,1:T(8,128)S(1)}, u32[]{:S(2)}, u32[]{:S(2)}) collective-permute-start(f32[8,18,1,512]{3,0,2,1:T(8,128)S(1)} %get-tuple-element.17), channel_id=1, source_target_pairs={{0,1},{1,2},{2,3},{3,4},{4,5},{5,6},{6,7},{7,0},{8,9},{9,10},{10,1... | collective-permute-start | bytes 884744 | tf_op jit(solution)/shard_map/ppermute | solution.py:15
  97.9 5.3 %copy-start.10 = (f32[8,18,1,512]{3,0,2,1:T(8,128)}, f32[8,18,1,512]{3,0,2,1:T(8,128)S(1)}, u32[]{:S(2)}) copy-start(f32[8,18,1,512]{3,0,2,1:T(8,128)S(1)} %collective-permute-done.10) | copy-start | bytes 884740
  103.2 0.7 copy-start.13
  114.0 11.3 %collective-permute-start.12 = (f32[8,1,16,512]{3,0,2,1:T(8,128)S(1)}, f32[8,1,16,512]{3,0,2,1:T(8,128)S(1)}, u32[]{:S(2)}, u32[]{:S(2)}) collective-permute-start(f32[8,1,16,512]{3,0,2,1:T(8,128)S(1)} %get-tuple-element.23), channel_id=1, source_target_pairs={{8,0},{16,8},{24,16},{0,24},{9,1},{17,9},{25,17},{1,25},{10,2},{18... | collective-permute-start | bytes 786440 | tf_op jit(solution)/shard_map/ppermute | solution.py:18
  117.1 11.6 %copy-start = (f32[8,16,16,512]{3,0,2,1:T(8,128)S(1)}, f32[8,16,16,512]{3,0,2,1:T(8,128)}, u32[]{:S(2)}) copy-start(f32[8,16,16,512]{3,0,2,1:T(8,128)} %fusion.15) | copy-start | bytes 12582916
  117.1 11.6 %collective-permute-start.13 = (f32[8,1,16,512]{3,0,2,1:T(8,128)S(1)}, f32[8,1,16,512]{3,0,2,1:T(8,128)S(1)}, u32[]{:S(2)}, u32[]{:S(2)}) collective-permute-start(f32[8,1,16,512]{3,0,2,1:T(8,128)S(1)} %get-tuple-element.22), channel_id=1, source_target_pairs={{0,8},{8,16},{16,24},{24,0},{1,9},{9,17},{17,25},{25,1},{2,10},{10... | collective-permute-start | bytes 786440 | tf_op jit(solution)/shard_map/ppermute | solution.py:15
  125.3 12.8 %copy-start.2 = (f32[8,16,16,512]{3,2,1,0:T(8,128)S(1)}, f32[8,16,16,512]{3,2,1,0:T(8,128)}, u32[]{:S(2)}) copy-start(f32[8,16,16,512]{3,2,1,0:T(8,128)} %param.4) | copy-start | bytes 12582916
  128.8 6.7 %collective-permute-start.14 = (f32[8,18,1,512]{3,0,2,1:T(8,128)S(1)}, f32[8,18,1,512]{3,0,2,1:T(8,128)S(1)}, u32[]{:S(2)}, u32[]{:S(2)}) collective-permute-start(f32[8,18,1,512]{3,0,2,1:T(8,128)S(1)} %get-tuple-element.14), channel_id=1, source_target_pairs={{1,0},{2,1},{3,2},{4,3},{5,4},{6,5},{7,6},{0,7},{9,8},{10,9},{11,1... | collective-permute-start | bytes 884744 | tf_op jit(solution)/shard_map/ppermute | solution.py:18
  128.8 9.3 %collective-permute-start.15 = (f32[8,18,1,512]{3,0,2,1:T(8,128)S(1)}, f32[8,18,1,512]{3,0,2,1:T(8,128)S(1)}, u32[]{:S(2)}, u32[]{:S(2)}) collective-permute-start(f32[8,18,1,512]{3,0,2,1:T(8,128)S(1)} %get-tuple-element.15), channel_id=1, source_target_pairs={{0,1},{1,2},{2,3},{3,4},{4,5},{5,6},{6,7},{7,0},{8,9},{9,10},{10,1... | collective-permute-start | bytes 884744 | tf_op jit(solution)/shard_map/ppermute | solution.py:15
where the time goes:
time: 199 us
  waiting for transfers between devices  51.7 us (26%)
  local copies, waits for them, and re-layouts  43.6 us (22%)
  other arithmetic  43 us (22%)
  blocking collectives  40.1 us (20%)
  starting transfers between devices  18.3 us (9%)
  between operations  2.17 us (1%)
    psum x1, blocking collectives, local(): stacked = lax.psum(stacked, ('gx', 'gy'))  40.1 us
    ppermute x8, waiting for transfers between devices, extended(): lax.ppermute(lax.slice_in_dim(block, 0, width, axis=dim), axis, backward)  26.7 us
    ppermute x8, waiting for transfers between devices, extended(): lax.ppermute(lax.slice_in_dim(block, block.shape[dim] - width, None, axis...  25 us
    slice x8, local copies, waits for them, and re-layouts, scaled_apply(): beside = beside + jnp.roll(core, 1, 3) + jnp.roll(core, -1, 3)  23 us
    sub x2, other arithmetic, local(): t_next = 2.0 * scaled_apply(with_rim(t_high), energy, center, width) - t_low  21.1 us
    unnamed x33, local copies, waits for them, and re-layouts  19.4 us
    ppermute x8, starting transfers between devices, extended(): lax.ppermute(lax.slice_in_dim(block, 0, width, axis=dim), axis, backward)  14.1 us
    reduce_sum x1, other arithmetic, inner_pair(): cross = jnp.sum(t_high * t_low, axis=(1, 2, 3))  13.2 us
  transfers between devices with their start and end apart: 16, of which 15 were waited for; matrix products, arithmetic and copies ran while one was open for 13% of the time, Pallas kernels for 0%

commit v1 on v0

v1 whole, which is shorter than its diff:
```python
import functools

import jax
import jax.numpy as jnp
from jax import lax
from jax.experimental import pallas as pl
from jax.experimental.pallas import tpu as pltpu
from jax.sharding import PartitionSpec as P

STEPS = 4
MESH = pl.DeviceIdType.MESH
ROWS = 8


def kernel(counts, sites, probes_hbm, disorder, center, width, last, moments, *scratch):
    fields = scratch[:STEPS]
    (near, faces, coef, acc, gather_x, gather_y, load_sem, send_sem, recv_sem,
     xs_sem, xr_sem, ys_sem, yr_sem) = scratch[STEPS:]
    n_probes, nx, ny, nz = probes_hbm.shape
    tiles = ny // ROWS
    count_x, count_y = counts
    me_x = lax.axis_index("gx")
    me_y = lax.axis_index("gy")

    def at_x(offset):
        return (lax.rem(me_x + offset, count_x), me_y)

    def at_y(offset):
        return (me_x, lax.rem(me_y + offset, count_y))

    def load(p):
        return pltpu.make_async_copy(
            probes_hbm.at[p], fields[0].at[p, pl.ds(1, nx)], load_sem.at[p])

    def x_sends(s, p):
        if s == 0:
            low, high = probes_hbm.at[p, 0], probes_hbm.at[p, nx - 1]
        else:
            low, high = fields[s].at[p, 1], fields[s].at[p, nx]
        return (
            pltpu.make_async_remote_copy(
                low, fields[s].at[p, nx + 1], send_sem.at[s, p, 0], recv_sem.at[s, p, 0],
                device_id=at_x(count_x - 1), device_id_type=MESH),
            pltpu.make_async_remote_copy(
                high, fields[s].at[p, 0], send_sem.at[s, p, 1], recv_sem.at[s, p, 1],
                device_id=at_x(1), device_id_type=MESH),
        )

    def y_sends(s, p):
        return (
            pltpu.make_async_remote_copy(
                faces.at[s, 0, p], near.at[s, 1, p], send_sem.at[s, p, 2], recv_sem.at[s, p, 2],
                device_id=at_y(count_y - 1), device_id_type=MESH),
            pltpu.make_async_remote_copy(
                faces.at[s, 1, p], near.at[s, 0, p], send_sem.at[s, p, 3], recv_sem.at[s, p, 3],
                device_id=at_y(1), device_id_type=MESH),
        )

    @pl.loop(0, n_probes)
    def _(p):
        load(p).start()

    barrier = pltpu.get_barrier_semaphore()
    for offset in range(1, count_x):
        pl.semaphore_signal(barrier, inc=1, device_id=at_x(offset), device_id_type=MESH)
    for offset in range(1, count_y):
        pl.semaphore_signal(barrier, inc=1, device_id=at_y(offset), device_id_type=MESH)

    scale = 2.0 / jnp.full((ROWS, nz), width[0], jnp.float32)
    middle = center[0]

    @pl.loop(0, nx)
    def _(x):
        for i in range(tiles):
            part = pl.ds(ROWS * i, ROWS)
            coef[x, part] = (disorder[x, part] - middle) * scale

    pl.semaphore_wait(barrier, count_x + count_y - 2)

    @pl.loop(0, n_probes)
    def _(p):
        for copy in x_sends(0, p):
            copy.start()

    @pl.loop(0, n_probes)
    def _(p):
        load(p).wait()

        @pl.loop(0, nx)
        def _(x):
            faces[0, 0, p, x] = fields[0][p, x + 1, pl.ds(0, 1)]
            faces[0, 1, p, x] = fields[0][p, x + 1, pl.ds(ny - 1, 1)]

        for copy in y_sends(0, p):
            copy.start()

    sub = lax.broadcasted_iota(jnp.int32, (ROWS, nz), 0)
    first = sub == 0
    final = sub == ROWS - 1
    lanes = lax.broadcasted_iota(jnp.int32, (n_probes, 128), 1)
    sums = jnp.zeros((n_probes, 128), jnp.float32)

    def fold(v):
        parts = [v[:, 128 * j:128 * (j + 1)] for j in range(nz // 128)]
        while len(parts) > 1:
            parts = [a + b for a, b in zip(parts[::2], parts[1::2])] + (
                [parts[-1]] if len(parts) % 2 else [])
        return parts[0]

    for s in range(STEPS):
        cur = fields[s]

        @pl.loop(0, n_probes)
        def _(p):
            for copy in x_sends(s, p) + y_sends(s, p):
                copy.wait_recv()

            def row(x, carry):
                square, cross = carry
                low = jnp.broadcast_to(near[s, 0, p, x], (ROWS, nz))
                high = jnp.broadcast_to(near[s, 1, p, x], (ROWS, nz))
                here = [cur[p, x + 1, pl.ds(ROWS * i, ROWS)] for i in range(tiles)]
                down = [pltpu.roll(v, 1, 0) for v in here]
                up = [pltpu.roll(v, ROWS - 1, 0) for v in here]
                for i in range(tiles):
                    part = pl.ds(ROWS * i, ROWS)
                    v = here[i]
                    below = jnp.where(first, low if i == 0 else down[i - 1], down[i])
                    above = jnp.where(final, high if i == tiles - 1 else up[i + 1], up[i])
                    beside = cur[p, x, part] + cur[p, x + 2, part]
                    beside = beside + (below + above)
                    beside = beside + (pltpu.roll(v, 1, 1) + pltpu.roll(v, nz - 1, 1))
                    new = coef[x, part] * v - scale * beside
                    if s == 0:
                        new = 0.5 * new
                    else:
                        new = new - fields[s - 1][p, x + 1, part]
                    if s + 1 < STEPS:
                        fields[s + 1][p, x + 1, part] = new
                        if i == 0:
                            faces[s + 1, 0, p, x] = new[0:1]
                        if i == tiles - 1:
                            faces[s + 1, 1, p, x] = new[ROWS - 1:ROWS]
                    else:
                        last[p, x, part] = new
                    square = square + fold(v * v)
                    cross = cross + fold(new * v)
                return square, cross

            zero = jnp.zeros((ROWS, 128), jnp.float32)
            square, cross = lax.fori_loop(0, nx, row, (zero, zero))
            acc[0, p] = square
            acc[1, p] = cross
            if s + 1 < STEPS:
                for copy in x_sends(s + 1, p) + y_sends(s + 1, p):
                    copy.start()

        for k in range(2):
            total = jnp.sum(jnp.sum(acc[k], axis=1), axis=1, keepdims=True)
            sums = sums + jnp.where(lanes == 2 * s + k, total, 0.0)

    def reduce_over(value, gather, sends, recvs, me, count, where):
        gather[me] = value

        def send(offset):
            return pltpu.make_async_remote_copy(
                gather.at[me], gather.at[me], sends.at[offset], recvs.at[me],
                device_id=where(offset), device_id_type=MESH)

        for offset in range(1, count):
            send(offset).start()
        for offset in range(1, count):
            source = lax.rem(me + offset, count)
            pltpu.make_async_remote_copy(
                gather.at[source], gather.at[source], sends.at[offset], recvs.at[source],
                device_id=where(offset), device_id_type=MESH).wait_recv()
        total = gather[0]
        for k in range(1, count):
            total = total + gather[k]
        return total, send

    sums, send_x = reduce_over(sums, gather_x, xs_sem, xr_sem, me_x, count_x, at_x)
    sums, send_y = reduce_over(sums, gather_y, ys_sem, yr_sem, me_y, count_y, at_y)
    mean = sums / jnp.float32(sites)
    start = jnp.where(lax.rem(lanes, 2) == 0, mean[:, 0:1], mean[:, 1:2])
    moments[...] = (2.0 * mean - start)[:, :2 * STEPS]

    for offset in range(1, count_x):
        send_x(offset).wait_send()
    for offset in range(1, count_y):
        send_y(offset).wait_send()
    for s in range(STEPS):
        @pl.loop(0, n_probes)
        def _(p):
            for copy in x_sends(s, p) + y_sends(s, p):
                copy.wait_send()


def local(counts, probes, disorder, spectrum_center, half_width):
    n_probes, nx, ny, nz = probes.shape
    sites = nx * counts[0] * ny * counts[1] * nz
    f32 = jnp.float32
    dma = pltpu.SemaphoreType.DMA
    vmem = pl.BlockSpec(memory_space=pltpu.VMEM)
    smem = pl.BlockSpec(memory_space=pltpu.SMEM)
    return pl.pallas_call(
        functools.partial(kernel, counts, sites),
        out_shape=(
            jax.ShapeDtypeStruct(probes.shape, f32),
            jax.ShapeDtypeStruct((n_probes, 2 * STEPS), f32),
        ),
        in_specs=[pl.BlockSpec(memory_space=pl.ANY), vmem, smem, smem],
        out_specs=(vmem, vmem),
        scratch_shapes=[pltpu.VMEM((n_probes, nx + 2, ny, nz), f32)] * STEPS + [
            pltpu.VMEM((STEPS, 2, n_probes, nx, 1, nz), f32),
            pltpu.VMEM((STEPS, 2, n_probes, nx, 1, nz), f32),
            pltpu.VMEM((nx, ny, nz), f32),
            pltpu.VMEM((2, n_probes, ROWS, 128), f32),
            pltpu.VMEM((counts[0], n_probes, 128), f32),
            pltpu.VMEM((counts[1], n_probes, 128), f32),
            dma((n_probes,)),
            dma((STEPS, n_probes, 4)),
            dma((STEPS, n_probes, 4)),
            dma((counts[0],)),
            dma((counts[0],)),
            dma((counts[1],)),
            dma((counts[1],)),
        ],
        compiler_params=pltpu.CompilerParams(
            collective_id=0, has_side_effects=True, vmem_limit_bytes=58 * 1024 * 1024),
        name="moments",
    )(probes, disorder, spectrum_center, half_width)


def solution(mesh):
    counts = (mesh.shape["gx"], mesh.shape["gy"])
    in_specs = (P(None, "gx", "gy", None), P("gx", "gy", None), P(), P())
    out_specs = (P(None, "gx", "gy", None), P())
    return jax.shard_map(functools.partial(local, counts), mesh=mesh, in_specs=in_specs,
                         out_specs=out_specs, check_vma=False)
```

time: 199 us -> 80.1 us (0.40)
  Pallas kernels: 0 us -> 72.3 us
  waiting for transfers between devices: 51.7 us -> 0 us
  other arithmetic: 43 us -> 0 us
  blocking collectives: 40.1 us -> 0 us
  local copies, waits for them, and re-layouts: 43.6 us -> 5.64 us
  starting transfers between devices: 18.3 us -> 0 us
    pallas_call x0 -> x1, Pallas kernels: none -> 72.3 us  [local(): pl.pallas_call(functools.partial(kernel, counts, sites), out_shape=(jax.S...]
    ppermute x16 -> x0, waiting for transfers between devices: 51.7 us -> none  [the longest x8 26.7 us: extended(): lax.ppermute(lax.slice_in_dim(block, 0, width, axis=dim), axis, backward)]
    psum x1 -> x0, blocking collectives: 40.1 us -> none  [local(): stacked = lax.psum(stacked, ('gx', 'gy'))]
    slice x14 -> x0, local copies, waits for them, and re-layouts: 24.2 us -> none  [the longest x8 23 us: scaled_apply(): beside = beside + jnp.roll(core, 1, 3) + jnp.roll(core, -1, 3)]
    sub x4 -> x0, other arithmetic: 21.1 us -> none  [the longest x2 21.1 us: local(): t_next = 2.0 * scaled_apply(with_rim(t_high), energy, center, width) - t_low]
    ppermute x16 -> x0, starting transfers between devices: 18.3 us -> none  [the longest x8 14.1 us: extended(): lax.ppermute(lax.slice_in_dim(block, 0, width, axis=dim), axis, backward)]
    unnamed x33 -> x4, local copies, waits for them, and re-layouts: 19.4 us -> 5.64 us
    reduce_sum x2 -> x0, other arithmetic: 13.7 us -> none  [the longest x1 13.2 us: inner_pair(): cross = jnp.sum(t_high * t_low, axis=(1, 2, 3))]
  transfers between devices with their start and end apart: 16 -> 0, of which waited for: 15 -> 0; matrix products, arithmetic and copies ran while one was open for 13% -> 0% of each run, Pallas kernels for 0% -> 0%
where the time goes in v1:
time: 80.1 us; the launch traced here: 79.9 us
  Pallas kernels  72.3 us (90%)
  local copies, waits for them, and re-layouts  5.64 us (7%)
  between operations  1.94 us (2%)
    pallas_call x1, Pallas kernels, local(): pl.pallas_call(functools.partial(kernel, counts, sites), out_shape=(jax.S...  72.3 us
    unnamed x4, local copies, waits for them, and re-layouts  5.64 us

profile of v1, /device:TPU:0, one launch (start us, length us, event | category | flops | bytes accessed | tf_op | source)
XLA Modules:
  0.0 79.9 jit_solution(5430660949732157242)
XLA Ops:
  1.9 72.3 %moments.1 = (f32[8,16,16,512]{3,2,1,0:T(8,128)}, f32[8,8]{1,0:T(8,128)}) custom-call(f32[8,16,16,512]{3,2,1,0:T(8,128)} %probes_hbm.1, f32[16,16,512]{2,1,0:T(8,128)} %disorder.1, f32[1]{0:T(128)S(6)} %copy.8.center, f32[1]{0:T(128)S(6)} %copy.9.width), custom_call_target="tpu_custom_call" | custom-call | tf_op jit(solution)/shard_map/moments/pallas_call | solution.py:206
  74.3 0.0 copy-start
  74.3 5.0 %copy.10 = f32[8,16,16,512]{3,2,1,0:T(8,128)} copy(f32[8,16,16,512]{3,2,1,0:T(8,128)} %get-tuple-element.4) | data formatting | bytes 8388608
  79.3 0.0 copy-done
  79.3 0.6 copy.11
Async XLA Ops:
  74.3 5.1 %copy-start = (f32[8,8]{1,0:T(8,128)S(1)}, f32[8,8]{1,0:T(8,128)}, u32[]{:S(2)}) copy-start(f32[8,8]{1,0:T(8,128)} %get-tuple-element.5) | copy-start | bytes 772

commit v2 on v1

--- a/solution.py
+++ b/solution.py
@@ -12,9 +12,9 @@
 ROWS = 8
 
 
-def kernel(counts, sites, probes_hbm, disorder, center, width, last, moments, *scratch):
+def kernel(counts, sites, probes_hbm, disorder_hbm, center, width, last_hbm, moments, *scratch):
     fields = scratch[:STEPS]
-    (near, faces, coef, acc, gather_x, gather_y, load_sem, send_sem, recv_sem,
+    (last, disorder, near, faces, coef, acc, gather_x, gather_y, load_sem, out_sem, energy_sem, send_sem, recv_sem,
      xs_sem, xr_sem, ys_sem, yr_sem) = scratch[STEPS:]
     n_probes, nx, ny, nz = probes_hbm.shape
     tiles = ny // ROWS
@@ -32,6 +32,9 @@
         return pltpu.make_async_copy(
             probes_hbm.at[p], fields[0].at[p, pl.ds(1, nx)], load_sem.at[p])
 
+    def store(p):
+        return pltpu.make_async_copy(last.at[p], last_hbm.at[p], out_sem.at[p])
+
     def x_sends(s, p):
         if s == 0:
             low, high = probes_hbm.at[p, 0], probes_hbm.at[p, nx - 1]
@@ -56,43 +59,47 @@
                 device_id=at_y(1), device_id_type=MESH),
         )
 
-    @pl.loop(0, n_probes)
-    def _(p):
-        load(p).start()
-
     barrier = pltpu.get_barrier_semaphore()
     for offset in range(1, count_x):
         pl.semaphore_signal(barrier, inc=1, device_id=at_x(offset), device_id_type=MESH)
     for offset in range(1, count_y):
         pl.semaphore_signal(barrier, inc=1, device_id=at_y(offset), device_id_type=MESH)
 
+    @pl.loop(0, n_probes)
+    def _(p):
+        load(p).start()
+
+    energy = pltpu.make_async_copy(disorder_hbm, disorder, energy_sem)
+    energy.start()
     scale = 2.0 / jnp.full((ROWS, nz), width[0], jnp.float32)
     middle = center[0]
+
+    pl.semaphore_wait(barrier, count_x + count_y - 2)
+
+    @pl.loop(0, n_probes)
+    def _(p):
+        for copy in x_sends(0, p):
+            copy.start()
+
+    @pl.loop(0, n_probes)
+    def _(p):
+        load(p).wait()
+
+        @pl.loop(0, nx)
+        def _(x):
+            faces[0, 0, p, x] = fields[0][p, x + 1, pl.ds(0, 1)]
+            faces[0, 1, p, x] = fields[0][p, x + 1, pl.ds(ny - 1, 1)]
+
+        for copy in y_sends(0, p):
+            copy.start()
+
+    energy.wait()
 
     @pl.loop(0, nx)
     def _(x):
         for i in range(tiles):
             part = pl.ds(ROWS * i, ROWS)
             coef[x, part] = (disorder[x, part] - middle) * scale
-
-    pl.semaphore_wait(barrier, count_x + count_y - 2)
-
-    @pl.loop(0, n_probes)
-    def _(p):
-        for copy in x_sends(0, p):
-            copy.start()
-
-    @pl.loop(0, n_probes)
-    def _(p):
-        load(p).wait()
-
-        @pl.loop(0, nx)
-        def _(x):
-            faces[0, 0, p, x] = fields[0][p, x + 1, pl.ds(0, 1)]
-            faces[0, 1, p, x] = fields[0][p, x + 1, pl.ds(ny - 1, 1)]
-
-        for copy in y_sends(0, p):
-            copy.start()
 
     sub = lax.broadcasted_iota(jnp.int32, (ROWS, nz), 0)
     first = sub == 0
@@ -148,12 +155,16 @@
                 return square, cross
 
             zero = jnp.zeros((ROWS, 128), jnp.float32)
-            square, cross = lax.fori_loop(0, nx, row, (zero, zero))
+            square, cross = lax.fori_loop(0, nx, row, (zero, zero), unroll=16)
             acc[0, p] = square
             acc[1, p] = cross
             if s + 1 < STEPS:
                 for copy in x_sends(s + 1, p) + y_sends(s + 1, p):
                     copy.start()
+            else:
+                store(p).start()
+            for copy in x_sends(s, p) + y_sends(s, p):
+                copy.wait_send()
 
         for k in range(2):
             total = jnp.sum(jnp.sum(acc[k], axis=1), axis=1, keepdims=True)
@@ -189,11 +200,10 @@
         send_x(offset).wait_send()
     for offset in range(1, count_y):
         send_y(offset).wait_send()
-    for s in range(STEPS):
-        @pl.loop(0, n_probes)
-        def _(p):
-            for copy in x_sends(s, p) + y_sends(s, p):
-                copy.wait_send()
+
+    @pl.loop(0, n_probes)
+    def _(p):
+        store(p).wait()
 
 
 def local(counts, probes, disorder, spectrum_center, half_width):
@@ -202,6 +212,7 @@
     f32 = jnp.float32
     dma = pltpu.SemaphoreType.DMA
     vmem = pl.BlockSpec(memory_space=pltpu.VMEM)
+    hbm = pl.BlockSpec(memory_space=pl.ANY)
     smem = pl.BlockSpec(memory_space=pltpu.SMEM)
     return pl.pallas_call(
         functools.partial(kernel, counts, sites),
@@ -209,9 +220,11 @@
             jax.ShapeDtypeStruct(probes.shape, f32),
             jax.ShapeDtypeStruct((n_probes, 2 * STEPS), f32),
         ),
-        in_specs=[pl.BlockSpec(memory_space=pl.ANY), vmem, smem, smem],
-        out_specs=(vmem, vmem),
+        in_specs=[hbm, hbm, smem, smem],
+        out_specs=(hbm, vmem),
         scratch_shapes=[pltpu.VMEM((n_probes, nx + 2, ny, nz), f32)] * STEPS + [
+            pltpu.VMEM(probes.shape, f32),
+            pltpu.VMEM((nx, ny, nz), f32),
             pltpu.VMEM((STEPS, 2, n_probes, nx, 1, nz), f32),
             pltpu.VMEM((STEPS, 2, n_probes, nx, 1, nz), f32),
             pltpu.VMEM((nx, ny, nz), f32),
@@ -219,6 +232,8 @@
             pltpu.VMEM((counts[0], n_probes, 128), f32),
             pltpu.VMEM((counts[1], n_probes, 128), f32),
             dma((n_probes,)),
+            dma((n_probes,)),
+            dma,
             dma((STEPS, n_probes, 4)),
             dma((STEPS, n_probes, 4)),
             dma((counts[0],)),

time: 80.1 us -> 71.4 us (0.89)
  Pallas kernels: 72.3 us -> 63.6 us
    pallas_call x1, Pallas kernels: 72.3 us -> 63.6 us  [local(): pl.pallas_call(functools.partial(kernel, counts, sites), out_shape=(jax.S...]
where the time goes in v2:
time: 71.4 us; the launch traced here: 71.2 us
  Pallas kernels  63.6 us (89%)
  local copies, waits for them, and re-layouts  5.64 us (8%)
  between operations  1.94 us (3%)
    pallas_call x1, Pallas kernels, local(): pl.pallas_call(functools.partial(kernel, counts, sites), out_shape=(jax.S...  63.6 us
    unnamed x4, local copies, waits for them, and re-layouts  5.64 us

profile of v2, /device:TPU:0, one launch (start us, length us, event | category | flops | bytes accessed | tf_op | source)
XLA Modules:
  0.0 71.2 jit_solution(6071158801053007325)
XLA Ops:
  1.9 63.6 %moments.1 = (f32[8,16,16,512]{3,2,1,0:T(8,128)}, f32[8,8]{1,0:T(8,128)}) custom-call(f32[8,16,16,512]{3,2,1,0:T(8,128)} %probes_hbm.1, f32[16,16,512]{2,1,0:T(8,128)} %disorder_hbm.1, f32[1]{0:T(128)S(6)} %copy.8.center, f32[1]{0:T(128)S(6)} %copy.9.width), custom_call_target="tpu_custom_call" | custom-call | tf_op jit(solution)/shard_map/moments/pallas_call | solution.py:217
  65.5 0.0 copy-start
  65.5 5.0 %copy.10 = f32[8,16,16,512]{3,2,1,0:T(8,128)} copy(f32[8,16,16,512]{3,2,1,0:T(8,128)} %get-tuple-element.4) | data formatting | bytes 8388608
  70.6 0.0 copy-done
  70.6 0.6 copy.11
Async XLA Ops:
  65.5 5.1 %copy-start = (f32[8,8]{1,0:T(8,128)S(1)}, f32[8,8]{1,0:T(8,128)}, u32[]{:S(2)}) copy-start(f32[8,8]{1,0:T(8,128)} %get-tuple-element.5) | copy-start | bytes 772
